TPU v7x, 32 devices: a whole 2x2x4 slice. The times are simulated.
32 devices in a mesh: path: 4 (over y, core), fsdp: 8 (over z, x).
Axes of the slice: x: 2, y: 2, z: 4, core: 2. Of those that a mesh axis runs over, the one named last changes fastest.
Arguments:
- input_activation_matrix: bfloat16 [4, 1536, 2048], P('path', 'fsdp'), may hold values from -6 to 6
- output_sensitivity: bfloat16 [4, 1536, 2048], P('path', 'fsdp'), may hold values from -12 to 12
- trajectory_initial_parameters: bfloat16 [4, 8, 1024, 4096], P('path', None, 'fsdp'), may hold values from -6 to 6
- trajectory_gradient_average: bfloat16 [4, 8, 1024, 4096], P('path', None, 'fsdp'), may hold values from -0.19921875 to 0.19921875
- trajectory_squared_average: bfloat16 [4, 8, 1024, 4096], P('path', None, 'fsdp'), may hold values from 0.0009994507 to 0.099609375
- common_expert_parameters: float32 [8, 2, 1024, 4096], P('path', None, 'fsdp'), may hold values from -6 to 6
- outer_inertia: float32 [8, 2, 1024, 4096], P('path', None, 'fsdp'), may hold values from -0.4 to 0.4
- trajectory_membership: int32 [4, 8], replicated, may hold values from 0 to 1
- punctual_flags: int32 [4], replicated, may hold values 0 or 1
Outputs:
- refreshed_experts: float32 [8, 2, 1024, 4096], P('path', None, 'fsdp')
- refreshed_inertia: float32 [8, 2, 1024, 4096], P('path', None, 'fsdp')
- returned: bfloat16 [4, 8, 1024, 4096], P('path', None, 'fsdp')
All inputs are finite; a program needn't handle non-finite values.
Results may differ from a plain program's by a relative error of at most 0.0024.
Values may be sent and summed in bfloat16 or wider, within the bound.
A program may use at most 320 MiB of HBM per device.

v0:
```python
import jax
import jax.numpy as jnp
from jax import lax
from jax.sharding import PartitionSpec as P

UNIT = 1024
SETS = 8
STEP = 1000
BETA_ONE = 0.9
BETA_TWO = 0.999
ADAM_EPS = 1e-08
INNER_RATE = 0.05
DECAY = 0.1
GLOBAL_LEARNING = 0.7
INERTIA_FACTOR = 0.9


def adam_delta(grads, first, second, start):
    corr_one = 1.0 - BETA_ONE**STEP
    corr_two = 1.0 - BETA_TWO**STEP
    first_new = BETA_ONE * first.astype(jnp.float32) + (1.0 - BETA_ONE) * grads
    second_new = BETA_TWO * second.astype(jnp.float32) + (1.0 - BETA_TWO) * grads * grads
    direction = first_new / corr_one / (jnp.sqrt(second_new / corr_two) + ADAM_EPS)
    return (INNER_RATE * (direction + DECAY * start.astype(jnp.float32))).astype(jnp.bfloat16)


def per_device(
    input_activation_matrix,
    output_sensitivity,
    trajectory_initial_parameters,
    trajectory_gradient_average,
    trajectory_squared_average,
    common_expert_parameters,
    outer_inertia,
    trajectory_membership,
    punctual_flags,
):
    set_count = trajectory_initial_parameters.shape[1]
    local_units = trajectory_initial_parameters.shape[2]
    row_width = trajectory_initial_parameters.shape[3]
    features = row_width // 2
    unit_rows = trajectory_initial_parameters[0].reshape(set_count * local_units, row_width)
    in_rows = unit_rows[:, :features]
    out_rows = unit_rows[:, features:]
    input_scale = features ** (-0.5)
    hidden_scale = (SETS * UNIT) ** (-0.5)
    contract_last = (((1,), (1,)), ((), ()))
    contract_first = (((0,), (0,)), ((), ()))
    inputs = lax.all_gather(input_activation_matrix[0], "fsdp", axis=0, tiled=True)
    upstream = lax.all_gather(output_sensitivity[0], "fsdp", axis=0, tiled=True)
    preact = (
        lax.dot_general(inputs, in_rows, contract_last, preferred_element_type=jnp.float32)
        * input_scale
    )
    active, pullback = jax.vjp(jax.nn.gelu, preact)
    active_half = active.astype(jnp.bfloat16)
    back_active = (
        lax.dot_general(upstream, out_rows, contract_last, preferred_element_type=jnp.float32)
        * hidden_scale
    )
    back_preact = pullback(back_active)[0].astype(jnp.bfloat16)
    grad_in = (
        lax.dot_general(back_preact, inputs, contract_first, preferred_element_type=jnp.float32)
        * input_scale
    )
    grad_out = (
        lax.dot_general(active_half, upstream, contract_first, preferred_element_type=jnp.float32)
        * hidden_scale
    )
    grad_in, grad_out = (grad_in, grad_out)
    grads = jnp.concatenate([grad_in, grad_out], axis=1)
    first_rows = trajectory_gradient_average[0].reshape(set_count * local_units, row_width)
    second_rows = trajectory_squared_average[0].reshape(set_count * local_units, row_width)
    pseudo = adam_delta(grads, first_rows, second_rows, unit_rows).reshape(
        set_count, local_units, row_width
    )
    path_count = lax.axis_size("path")
    position = lax.axis_index("path")
    owned_sets = set_count // path_count
    choices = common_expert_parameters.shape[1]
    eligible_trajectories = jnp.arange(choices, dtype=jnp.int32)
    picked_trajectories = jnp.where(
        (trajectory_membership[:, :, None] == eligible_trajectories[None, None, :])
        & (punctual_flags[:, None, None] == 1),
        1.0,
        0.0,
    ).astype(jnp.float32)
    first_set = position * owned_sets
    owner_module_weights = lax.dynamic_slice_in_dim(picked_trajectories, first_set, owned_sets, 1)
    punctual_tally = jnp.sum(owner_module_weights, axis=0)
    own_weights = lax.dynamic_index_in_dim(picked_trajectories, position, 0, keepdims=False)
    contributions = own_weights[:, :, None, None] * pseudo.astype(jnp.float32)[:, None]
    aggregate_change = lax.psum_scatter(
        contributions.astype(jnp.bfloat16), "path", scatter_dimension=0, tiled=True
    ).astype(jnp.float32)
    punctual_average = aggregate_change / jnp.maximum(punctual_tally, 1.0)[:, :, None, None]
    refreshed_inertia = INERTIA_FACTOR * outer_inertia + punctual_average
    refreshed_experts = common_expert_parameters - GLOBAL_LEARNING * (
        punctual_average + INERTIA_FACTOR * refreshed_inertia
    )
    updated = refreshed_experts.astype(jnp.bfloat16)
    all_modules = lax.all_gather(updated, "path", axis=0, tiled=True)
    own_choice = lax.dynamic_index_in_dim(trajectory_membership, position, 0, keepdims=False)
    returned = jnp.take_along_axis(all_modules, own_choice[:, None, None, None], axis=1)[:, 0]
    return (refreshed_experts, refreshed_inertia, returned[None])


def solution(mesh):
    placed = (
        P("path", "fsdp", None),
        P("path", "fsdp", None),
        P("path", None, "fsdp", None),
        P("path", None, "fsdp", None),
        P("path", None, "fsdp", None),
        P("path", None, "fsdp", None),
        P("path", None, "fsdp", None),
        P(),
        P(),
    )
    return jax.shard_map(
        per_device,
        mesh=mesh,
        in_specs=placed,
        out_specs=(
            P("path", None, "fsdp", None),
            P("path", None, "fsdp", None),
            P("path", None, "fsdp", None),
        ),
        check_vma=False,
    )
```

profile of v0, /device:TPU:0, one launch (start us, length us, event | category | flops | bytes accessed | tf_op | source)
XLA Modules:
  0.0 543.5 jit_solution(6791174297192927239)
XLA Ops:
  7.2 0.0 all-gather.10.cloned.1.call-start
  7.2 0.7 all-gather.10.cloned.1.call-update
  7.9 0.0 all-gather.8.cloned.1.call-start
  7.9 0.7 all-gather.8.cloned.1.call-update
  8.6 0.0 reduce-scatter.2.cloned.1.call-start
  8.7 0.7 broadcast_compare_fusion
  9.4 0.8 and_select_fusion
  10.1 0.1 copy.13
  10.2 101.4 %all-gather.10.cloned.1.call-done = bf16[1,1536,2048]{2,1,0:T(8,128)(2,1)} async-done(((bf16[1,192,2048]{2,1,0:T(8,128)(2,1)}), bf16[1,1536,2048]{2,1,0:T(8,128)(2,1)}) %all-gather.10.cloned.1.call-update) | async-done | bytes 6291472 | tf_op jit(solution)/shard_map/all_gather | solution.py:49
  111.6 11.7 %fusion.16 = f32[1536,1024]{1,0:T(8,128)} fusion(bf16[1,1536,2048]{2,1,0:T(8,128)(2,1)} %all-gather.10.cloned.1.call-done, bf16[1024,4096]{1,0:T(8,128)(2,1)} %bitcast.53), kind=kOutput, calls=%fused_computation.28 | convolution fusion | flops 6442450944 | bytes 16777216 | tf_op jit(solution)/shard_map/dot_general | solution.py:52
  123.3 87.4 %all-gather.8.cloned.1.call-done = bf16[1,1536,2048]{2,1,0:T(8,128)(2,1)} async-done(((bf16[1,192,2048]{2,1,0:T(8,128)(2,1)}), bf16[1,1536,2048]{2,1,0:T(8,128)(2,1)}) %all-gather.8.cloned.1.call-update) | async-done | bytes 6291472 | tf_op jit(solution)/shard_map/all_gather | solution.py:50
  210.7 26.1 %fusion.27 = f32[1024,2048]{1,0:T(8,128)} fusion(bf16[1,1536,2048]{2,1,0:T(8,128)(2,1)} %all-gather.10.cloned.1.call-done, f32[1536,1024]{1,0:T(8,128)} %fusion.16, bf16[1,1536,2048]{2,1,0:T(8,128)(2,1)} %all-gather.8.cloned.1.call-done, bf16[1024,4096]{1,0:T(8,128)(2,1)} %bitcast.54), kind=kOutput, calls=%fused_computation.36 | convolution fusion | flops 12921602048 | bytes 31457280 | tf_op jit(solution)/shard_map/dot_general | solution.py:63
  236.8 13.7 %fusion.24 = f32[1024,2048]{1,0:T(8,128)} fusion(bf16[1,1536,2048]{2,1,0:T(8,128)(2,1)} %all-gather.8.cloned.1.call-done, f32[1536,1024]{1,0:T(8,128)} %fusion.16), kind=kOutput, calls=%fused_computation.35 | convolution fusion | flops 6460276736 | bytes 20971520 | tf_op jit(solution)/shard_map/dot_general | solution.py:67
  250.4 18.0 %fusion.6 = f32[8,128,4096]{2,1,0:T(8,128)S(1)} fusion(bf16[1,8,128,4096]{3,2,1,0:T(8,128)(2,1)} %param.11, bf16[1,8,128,4096]{3,2,1,0:T(8,128)(2,1)} %param.13, f32[8,128,2048]{2,1,0:T(8,128)} %bitcast.56, f32[8,128,2048]{2,1,0:T(8,128)} %bitcast.55, bf16[1,8,128,4096]{3,2,1,0:T(8,128)(2,1)} %param.12), kind=kLoop, calls=%fused_computation.18 | loop fusion | flops 79691776 | bytes 58720256 | tf_op jit(solution)/shard_map/convert_element_type | solution.py:92
  268.5 7.6 %multiply_convert_fusion = bf16[8,2,128,4096]{3,2,1,0:T(8,128)(2,1)} fusion(f32[8,128,4096]{2,1,0:T(8,128)S(1)} %fusion.6, f32[8,2]{1,0:T(8,128)S(1)} %copy.13), kind=kLoop, calls=%fused_computation.1 | loop fusion | flops 16777216 | bytes 33554496 | tf_op jit(solution)/shard_map/convert_element_type | solution.py:94
  276.1 0.0 reduce-scatter.2.cloned.1.call-update
  276.1 0.0 all-gather.6.cloned.1.call-start
  276.2 0.1 dynamic-slice_reduce_fusion
  276.3 0.1 copy.14
  276.4 0.0 copy-start
  276.4 123.2 %reduce-scatter.2.cloned.1.call-done = bf16[2,2,128,4096]{3,2,1,0:T(8,128)(2,1)} async-done(((bf16[8,2,128,4096]{3,2,1,0:T(8,128)(2,1)}), bf16[2,2,128,4096]{3,2,1,0:T(8,128)(2,1)}) %reduce-scatter.2.cloned.1.call-update) | async-done | bytes 4194320 | tf_op jit(solution)/shard_map/reduce_scatter | solution.py:93
  399.5 13.0 %fusion.62 = (bf16[2,2,128,4096]{3,2,1,0:T(8,128)(2,1)}, f32[2,2,128,4096]{3,2,1,0:T(8,128)}, f32[2,2,128,4096]{3,2,1,0:T(8,128)}) fusion(f32[2,2,128,4096]{3,2,1,0:T(8,128)} %param.14, f32[2,2]{1,0:T(2,128)S(1)} %copy.14, bf16[2,2,128,4096]{3,2,1,0:T(8,128)(2,1)} %reduce-scatter.2.cloned.1.call-done, f32[2,2,128,4096]{3,2,1,0:T(8,128)} %param.15), kind=kLoop, calls=%fused_computation.76 | loop fusion | flops 18874368 | bytes 41943056 | tf_op jit(solution)/shard_map/convert_element_type | solution.py:101
  412.6 0.0 all-gather.6.cloned.1.call-update
  412.6 0.0 copy-done
  412.7 106.0 %all-gather.6.cloned.1.call-done = bf16[8,2,128,4096]{3,2,1,0:T(8,128)(2,1)} async-done(((bf16[2,2,128,4096]{3,2,1,0:T(8,128)(2,1)}), bf16[8,2,128,4096]{3,2,1,0:T(8,128)(2,1)}) %all-gather.6.cloned.1.call-update) | async-done | bytes 16777232 | tf_op jit(solution)/shard_map/all_gather | solution.py:102
  518.6 10.7 %gather_fusion = bf16[8,128,4096]{2,1,0:T(8,128)(2,1)} fusion(bf16[8,2,128,4096]{3,2,1,0:T(8,128)(2,1)} %all-gather.6.cloned.1.call-done, s32[8]{0:T(128)S(1)} %or_bitcast_fusion), kind=kCustom, calls=%fused_computation | custom fusion | bytes 16777280 | tf_op jit(solution)/shard_map/jit(take_along_axis)/gather | solution.py:104
  529.3 7.6 %bitcast_select_fusion = bf16[1,8,128,4096]{3,2,1,0:T(8,128)(2,1)} fusion(bf16[8,128,4096]{2,1,0:T(8,128)(2,1)} %gather_fusion, pred[8]{0:T(512)(128)(4,1)S(1)} %compare_and_fusion), kind=kLoop, calls=%fused_computation.14 | loop fusion | flops 4194304 | bytes 16777224 | tf_op jit(solution)/shard_map/jit(take_along_axis)/select_n | solution.py:104
  (7 shorter events, 0.1 us)
Async XLA Ops:
  7.2 104.4 %all-gather.10.cloned.1.call-start = ((), (), s32[]{:S(2)}) async-start(), calls=%async_computation.4 | async-start | bytes 7077888 | tf_op jit(solution)/shard_map/all_gather | solution.py:49
  7.9 202.8 %all-gather.8.cloned.1.call-start = ((), (), s32[]{:S(2)}) async-start(), calls=%async_computation.3 | async-start | bytes 7077888 | tf_op jit(solution)/shard_map/all_gather | solution.py:50
  8.6 390.9 %reduce-scatter.2.cloned.1.call-start = ((), (), s32[]{:S(2)}) async-start(), calls=%async_computation.1 | async-start | bytes 20971520 | tf_op jit(solution)/shard_map/reduce_scatter | solution.py:93
  276.1 242.5 %all-gather.6.cloned.1.call-start = ((), (), s32[]{:S(2)}) async-start(), calls=%async_computation.2 | async-start | bytes 20971520 | tf_op jit(solution)/shard_map/all_gather | solution.py:102
  276.4 136.2 %copy-start = (s32[4,8]{1,0:T(4,128)S(1)}, s32[4,8]{1,0:T(4,128)}, u32[]{:S(2)}) copy-start(s32[4,8]{1,0:T(4,128)} %param.16) | copy-start | bytes 388
Sparse Core Ops, SparseCore 0:
  10.2 101.3 all-gather.9
  113.8 96.8 all-gather.7
  276.3 123.2 reduce-scatter.1
  412.7 105.8 all-gather.5
where the time goes:
time: 544 us; the launch traced here: 543 us
  waiting for transfers between devices  419 us (77%)
  matrix products  51.5 us (9%)
  other arithmetic  47.9 us (9%)
  between operations  13.8 us (3%)
  local copies, waits for them, and re-layouts  10.8 us (2%)
    reduce_scatter x1, waiting for transfers between devices, per_device(): lax.psum_scatter(contributions.astype(jnp.bfloat16), 'path', scatter_dime...  123 us
    all_gather x1, waiting for transfers between devices, per_device(): all_modules = lax.all_gather(updated, 'path', axis=0, tiled=True)  106 us
    all_gather x1, waiting for transfers between devices, per_device(): lax.all_gather(input_activation_matrix[0], 'fsdp', axis=0, tiled=True)  101 us
    all_gather x1, waiting for transfers between devices, per_device(): upstream = lax.all_gather(output_sensitivity[0], 'fsdp', axis=0, tiled=True)  87.4 us
    dot_general x1, matrix products, per_device(): lax.dot_general(back_preact, inputs, contract_first, preferred_element_ty...  26.1 us
    convert_element_type x1, other arithmetic, per_device(): pseudo.astype(jnp.float32)[:, None]  18 us
    dot_general x1, matrix products, per_device(): lax.dot_general(active_half, upstream, contract_first, preferred_element_...  13.7 us
    convert_element_type x1, other arithmetic, per_device(): updated = refreshed_experts.astype(jnp.bfloat16)  13 us
  transfers between devices with their start and end apart: 4, of which 4 were waited for; matrix products, arithmetic and copies ran while one was open for 2% of the time, Pallas kernels for 0%

commit v1 on v0

--- a/solution.py
+++ b/solution.py
@@ -47,7 +47,11 @@
     contract_last = (((1,), (1,)), ((), ()))
     contract_first = (((0,), (0,)), ((), ()))
     inputs = lax.all_gather(input_activation_matrix[0], "fsdp", axis=0, tiled=True)
-    upstream = lax.all_gather(output_sensitivity[0], "fsdp", axis=0, tiled=True)
+    row_data = output_sensitivity[0]
+    z2 = lax.axis_size("fsdp")
+    inter = jnp.stack([row_data] * z2)
+    state_next = lax.all_to_all(inter, "fsdp", 0, 0)
+    upstream = jnp.concatenate(state_next, axis=0)
     preact = (
         lax.dot_general(inputs, in_rows, contract_last, preferred_element_type=jnp.float32)
         * input_scale

time: 544 us -> 572 us (1.051)
  waiting for transfers between devices: 419 us -> 437 us
  starting transfers between devices: 0.16 us -> 7.4 us
    all_gather x1, waiting for transfers between devices: 101 us -> 207 us  [per_device(): lax.all_gather(input_activation_matrix[0], 'fsdp', axis=0, tiled=True)]
    all_gather x1 -> x0, waiting for transfers between devices: 87.4 us -> none  [per_device(): upstream = lax.all_gather(output_sensitivity[0], 'fsdp', axis=0, tiled=True)]
    all_to_all x0 -> x1, starting transfers between devices: none -> 7.28 us  [per_device(): state_next = lax.all_to_all(inter, 'fsdp', 0, 0)]
  transfers between devices with their start and end apart: 4 -> 4, of which waited for: 4 -> 3; matrix products, arithmetic and copies ran while one was open for 2% -> 3% of each run, Pallas kernels for 0% -> 0%
where the time goes in v1:
time: 572 us
  waiting for transfers between devices  437 us (76%)
  matrix products  51.5 us (9%)
  other arithmetic  46.8 us (8%)
  local copies, waits for them, and re-layouts  15.5 us (3%)
  between operations  13.8 us (2%)
  starting transfers between devices  7.4 us (1%)
    all_gather x1, waiting for transfers between devices, per_device(): lax.all_gather(input_activation_matrix[0], 'fsdp', axis=0, tiled=True)  207 us
    reduce_scatter x1, waiting for transfers between devices, per_device(): lax.psum_scatter(contributions.astype(jnp.bfloat16), 'path', scatter_dime...  123 us
    all_gather x1, waiting for transfers between devices, per_device(): all_modules = lax.all_gather(updated, 'path', axis=0, tiled=True)  106 us
    dot_general x1, matrix products, per_device(): lax.dot_general(back_preact, inputs, contract_first, preferred_element_ty...  26.1 us
    convert_element_type x1, other arithmetic, per_device(): pseudo.astype(jnp.float32)[:, None]  18 us
    dot_general x1, matrix products, per_device(): lax.dot_general(active_half, upstream, contract_first, preferred_element_...  13.7 us
    convert_element_type x1, other arithmetic, per_device(): updated = refreshed_experts.astype(jnp.bfloat16)  13 us
    dot_general x1, matrix products, per_device(): lax.dot_general(inputs, in_rows, contract_last, preferred_element_type=jn...  11.7 us
  transfers between devices with their start and end apart: 4, of which 3 were waited for; matrix products, arithmetic and copies ran while one was open for 3% of the time, Pallas kernels for 0%

profile of v1, /device:TPU:0, one launch (start us, length us, event | category | flops | bytes accessed | tf_op | source)
XLA Modules:
  0.0 571.6 jit_solution(6753261386714020467)
XLA Ops:
  7.2 0.0 all-gather.6.cloned.1.call-start
  7.2 0.7 all-gather.6.cloned.1.call-update
  7.9 0.0 copy-start.1
  7.9 0.0 copy-start
  7.9 4.6 stack.3
  12.6 7.3 %all-to-all-start = ((bf16[8,192,2048]{2,1,0:T(8,128)(2,1)}), bf16[8,192,2048]{2,1,0:T(8,128)(2,1)}, u32[]{:S(2)}, u32[]{:S(2)}) async-start(bf16[8,192,2048]{2,1,0:T(8,128)(2,1)} %stack.3), calls=%async_computation | async-start | bytes 12582912 | tf_op jit(solution)/shard_map/all_to_all | solution.py:53
  19.8 0.0 reduce-scatter.2.cloned.1.call-start
  19.9 0.0 copy-done.1
  19.9 0.0 copy-done
  19.9 0.1 and_select_fusion
  20.0 0.1 copy.13
  20.1 206.9 %all-gather.6.cloned.1.call-done = bf16[1,1536,2048]{2,1,0:T(8,128)(2,1)} async-done(((bf16[1,192,2048]{2,1,0:T(8,128)(2,1)}), bf16[1,1536,2048]{2,1,0:T(8,128)(2,1)}) %all-gather.6.cloned.1.call-update) | async-done | bytes 6291472 | tf_op jit(solution)/shard_map/all_gather | solution.py:49
  227.0 11.7 %fusion.16 = f32[1536,1024]{1,0:T(8,128)} fusion(bf16[1,1536,2048]{2,1,0:T(8,128)(2,1)} %all-gather.6.cloned.1.call-done, bf16[1024,4096]{1,0:T(8,128)(2,1)} %bitcast.46), kind=kOutput, calls=%fused_computation.28 | convolution fusion | flops 6442450944 | bytes 16777216 | tf_op jit(solution)/shard_map/dot_general | solution.py:56
  238.7 0.0 all-to-all-done
  238.7 13.7 %convolution_multiply_fusion = f32[1024,2048]{1,0:T(8,128)} fusion(bf16[1536,2048]{1,0:T(8,128)(2,1)} %bitcast.3, f32[1536,1024]{1,0:T(8,128)} %fusion.16), kind=kOutput, calls=%fused_computation.32 | convolution fusion | flops 6460276736 | bytes 20971520 | tf_op jit(solution)/shard_map/dot_general | solution.py:71
  252.4 26.1 %fusion.18 = f32[1024,2048]{1,0:T(8,128)} fusion(bf16[1,1536,2048]{2,1,0:T(8,128)(2,1)} %all-gather.6.cloned.1.call-done, f32[1536,1024]{1,0:T(8,128)} %fusion.16, bf16[1536,2048]{1,0:T(8,128)(2,1)} %bitcast.3, bf16[1024,4096]{1,0:T(8,128)(2,1)} %bitcast.47), kind=kOutput, calls=%fused_computation.31 | convolution fusion | flops 12921602048 | bytes 31457280 | tf_op jit(solution)/shard_map/dot_general | solution.py:67
  278.5 18.0 %fusion.6 = f32[8,128,4096]{2,1,0:T(8,128)S(1)} fusion(bf16[1,8,128,4096]{3,2,1,0:T(8,128)(2,1)} %param.11, bf16[1,8,128,4096]{3,2,1,0:T(8,128)(2,1)} %param.13, f32[8,128,2048]{2,1,0:T(8,128)} %bitcast.48, f32[8,128,2048]{2,1,0:T(8,128)} %bitcast.49, bf16[1,8,128,4096]{3,2,1,0:T(8,128)(2,1)} %param.12), kind=kLoop, calls=%fused_computation.18 | loop fusion | flops 79691776 | bytes 58720256 | tf_op jit(solution)/shard_map/convert_element_type | solution.py:96
  296.6 7.8 %multiply_convert_fusion = bf16[8,2,128,4096]{3,2,1,0:T(8,128)(2,1)} fusion(f32[8,128,4096]{2,1,0:T(8,128)S(1)} %fusion.6, f32[8,2]{1,0:T(8,128)S(1)} %copy.13), kind=kLoop, calls=%fused_computation.1 | loop fusion | flops 16777216 | bytes 33554496 | tf_op jit(solution)/shard_map/convert_element_type | solution.py:98
  304.4 0.0 reduce-scatter.2.cloned.1.call-update
  304.4 0.0 all-gather.4.cloned.1.call-start
  304.5 0.1 dynamic-slice_reduce_fusion
  304.6 0.1 copy.14
  304.7 123.0 %reduce-scatter.2.cloned.1.call-done = bf16[2,2,128,4096]{3,2,1,0:T(8,128)(2,1)} async-done(((bf16[8,2,128,4096]{3,2,1,0:T(8,128)(2,1)}), bf16[2,2,128,4096]{3,2,1,0:T(8,128)(2,1)}) %reduce-scatter.2.cloned.1.call-update) | async-done | bytes 4194320 | tf_op jit(solution)/shard_map/reduce_scatter | solution.py:97
  427.7 13.0 %fusion.51 = (bf16[2,2,128,4096]{3,2,1,0:T(8,128)(2,1)}, f32[2,2,128,4096]{3,2,1,0:T(8,128)}, f32[2,2,128,4096]{3,2,1,0:T(8,128)}) fusion(f32[2,2,128,4096]{3,2,1,0:T(8,128)} %param.14, f32[2,2]{1,0:T(2,128)S(1)} %copy.14, bf16[2,2,128,4096]{3,2,1,0:T(8,128)(2,1)} %reduce-scatter.2.cloned.1.call-done, f32[2,2,128,4096]{3,2,1,0:T(8,128)} %param.15), kind=kLoop, calls=%fused_computation.72 | loop fusion | flops 18874368 | bytes 41943056 | tf_op jit(solution)/shard_map/convert_element_type | solution.py:105
  440.7 0.0 all-gather.4.cloned.1.call-update
  440.8 106.0 %all-gather.4.cloned.1.call-done = bf16[8,2,128,4096]{3,2,1,0:T(8,128)(2,1)} async-done(((bf16[2,2,128,4096]{3,2,1,0:T(8,128)(2,1)}), bf16[8,2,128,4096]{3,2,1,0:T(8,128)(2,1)}) %all-gather.4.cloned.1.call-update) | async-done | bytes 16777232 | tf_op jit(solution)/shard_map/all_gather | solution.py:106
  546.8 10.7 %gather_fusion = bf16[8,128,4096]{2,1,0:T(8,128)(2,1)} fusion(bf16[8,2,128,4096]{3,2,1,0:T(8,128)(2,1)} %all-gather.4.cloned.1.call-done, s32[8]{0:T(128)S(1)} %or_bitcast_fusion), kind=kCustom, calls=%fused_computation | custom fusion | bytes 16777280 | tf_op jit(solution)/shard_map/jit(take_along_axis)/gather | solution.py:108
  557.4 7.6 %bitcast_select_fusion = bf16[1,8,128,4096]{3,2,1,0:T(8,128)(2,1)} fusion(bf16[8,128,4096]{2,1,0:T(8,128)(2,1)} %gather_fusion, pred[8]{0:T(512)(128)(4,1)S(1)} %compare_and_fusion), kind=kLoop, calls=%fused_computation.14 | loop fusion | flops 4194304 | bytes 16777224 | tf_op jit(solution)/shard_map/jit(take_along_axis)/select_n | solution.py:108
  (8 shorter events, 0.1 us)
Async XLA Ops:
  7.2 219.9 %all-gather.6.cloned.1.call-start = ((), (), s32[]{:S(2)}) async-start(), calls=%async_computation.4 | async-start | bytes 7077888 | tf_op jit(solution)/shard_map/all_gather | solution.py:49
  7.9 12.0 %copy-start.1 = (s32[4]{0:T(128)S(1)}, s32[4]{0:T(128)}, u32[]{:S(2)}) copy-start(s32[4]{0:T(128)} %param.17) | copy-start | bytes 52
  7.9 12.0 %copy-start = (s32[4,8]{1,0:T(4,128)S(1)}, s32[4,8]{1,0:T(4,128)}, u32[]{:S(2)}) copy-start(s32[4,8]{1,0:T(4,128)} %param.16) | copy-start | bytes 388
  12.6 226.2 %all-to-all-start = ((bf16[8,192,2048]{2,1,0:T(8,128)(2,1)}), bf16[8,192,2048]{2,1,0:T(8,128)(2,1)}, u32[]{:S(2)}, u32[]{:S(2)}) async-start(bf16[8,192,2048]{2,1,0:T(8,128)(2,1)} %stack.3), calls=%async_computation | async-start | bytes 12582912 | tf_op jit(solution)/shard_map/all_to_all | solution.py:53
  19.8 407.8 %reduce-scatter.2.cloned.1.call-start = ((), (), s32[]{:S(2)}) async-start(), calls=%async_computation.2 | async-start | bytes 20971520 | tf_op jit(solution)/shard_map/reduce_scatter | solution.py:97
  304.4 242.4 %all-gather.4.cloned.1.call-start = ((), (), s32[]{:S(2)}) async-start(), calls=%async_computation.3 | async-start | bytes 20971520 | tf_op jit(solution)/shard_map/all_gather | solution.py:106
Sparse Core Ops, SparseCore 0:
  10.2 216.8 all-gather.5
  304.5 123.0 reduce-scatter.1
  440.8 105.8 all-gather.3
